TPU v7x, 32 devices: a whole 2x2x4 slice. The times are simulated.
32 devices in a mesh: ens: 4 (over x, core), elem: 8 (over z, y).
Axes of the slice: x: 2, y: 2, z: 4, core: 2. Of those that a mesh axis runs over, the one named last changes fastest.
Arguments:
- scalars: float32 [8, 512, 1024], P('ens', None, 'elem'), parts along dimension 0, may hold values from -6 to 6
- transport: float32 [3, 512, 1024], P(None, None, 'elem'), may hold values from -6 to 6
- mass: float32 [512, 1024], P(None, 'elem'), may hold values from 0.5 to 2
- element_order: int32 [8, 128], P('elem'), may hold values from 0 to 127, each once within a row
Outputs:
- advected: float32 [8, 512, 1024], P('ens', None, 'elem'), parts along dimension 0
There are 4 independent parts, one for each index of `ens`. A program takes and returns all parts, laid end to end along the dimension named above; an argument that names none is the same for every part. Nothing has to cross between parts.
Inputs may be any that keep to these rules, and one draw needn't show every extreme that they name: `element_order`: each row is a permutation of the device's slots.
All inputs are finite; a program needn't handle non-finite values.
Results may differ from a plain program's by a relative error of at most 0.0001.
Values sent between devices are 32-bit elements; how exact they have to be, the bound alone decides.
A program may use at most 64 MiB of HBM per device.

v0:
```python
import functools

import jax
import jax.numpy as jnp
import numpy as np
from jax import lax
from jax.experimental import pallas as pl
from jax.experimental.pallas import tpu as pltpu
from jax.sharding import PartitionSpec as P

ORDER = 7
SUBSTEPS = 2
EX = 1
EY = 8
EZ = 16
EXTENT = ORDER + 1
PLANE = EXTENT * EXTENT
NODES = EXTENT * PLANE
MESH = pl.DeviceIdType.MESH


time_step = 0.015


def legendre_table(points, degree):
    table = np.zeros((points.shape[0], degree + 1))
    table[:, 0] = 1.0
    table[:, 1] = points
    for level in range(2, degree + 1):
        table[:, level] = (
            (2 * level - 1) * points * table[:, level - 1] - (level - 1) * table[:, level - 2]
        ) / level
    return table


def gll_derivative(degree):
    extent = degree + 1
    points = np.cos(np.pi * np.arange(extent) / degree)
    for sweep in range(60):
        table = legendre_table(points, degree)
        points = points - (points * table[:, degree] - table[:, degree - 1]) / (
            extent * table[:, degree]
        )
    points = points[::-1].copy()
    values = legendre_table(points, degree)[:, degree]
    matrix = np.zeros((extent, extent))
    for target in range(extent):
        for source in range(extent):
            if target != source:
                matrix[target, source] = values[target] / (
                    values[source] * (points[target] - points[source])
                )
    matrix[0, 0] = -degree * (degree + 1) / 4.0
    matrix[extent - 1, extent - 1] = degree * (degree + 1) / 4.0
    return matrix


def split_matrix():
    derivative = gll_derivative(ORDER).astype(np.float32)
    eye = np.eye(EXTENT, dtype=np.float32)
    full = np.concatenate([np.kron(derivative, eye), np.kron(eye, derivative)], axis=0)
    high = full.astype(jnp.bfloat16)
    low = (full - high.astype(np.float32)).astype(jnp.bfloat16)
    return np.concatenate([high, high, low], axis=1)


def halves(values):
    high = values.astype(jnp.bfloat16)
    low = (values - high.astype(jnp.float32)).astype(jnp.bfloat16)
    return high, low


def lane_forward(values, stride, length):
    total = values.shape[-1]
    near = pltpu.roll(values, total - stride, 1)
    if stride * length == total:
        return near
    coords = lax.broadcasted_iota(jnp.int32, values.shape, 1) // stride % length
    return jnp.where(coords < length - 1, near, pltpu.roll(values, stride * (length - 1), 1))


def lane_backward(values, stride, length):
    total = values.shape[-1]
    near = pltpu.roll(values, stride, 1)
    if stride * length == total:
        return near
    coords = lax.broadcasted_iota(jnp.int32, values.shape, 1) // stride % length
    return jnp.where(coords > 0, near, pltpu.roll(values, total - stride * (length - 1), 1))


def store_assembled(ref, row, values):
    low, high = values[:EXTENT], values[PLANE - EXTENT :]
    ref[row : row + EXTENT] = low + lane_backward(high, EZ, EY)
    ref[row + EXTENT : row + PLANE - EXTENT] = values[EXTENT : PLANE - EXTENT]
    ref[row + PLANE - EXTENT : row + PLANE] = high + lane_forward(low, EZ, EY)
    first = pl.ds(row, EXTENT, stride=EXTENT)
    last = pl.ds(row + ORDER, EXTENT, stride=EXTENT)
    k_low = ref[first, :]
    k_high = ref[last, :]
    ref[first, :] = k_low + lane_backward(k_high, 1, EZ)
    ref[last, :] = k_high + lane_forward(k_low, 1, EZ)


def kernel(
    count, members, scalars, transport, mass, order, matrix, out,
    speed, current, base, total, work, inverse, send, recv, send_sem, recv_sem,
):
    me = lax.axis_index("elem")
    right, left = lax.rem(me + 1, count), lax.rem(me + count - 1, count)
    barrier = pltpu.get_barrier_semaphore()
    for neighbour in (left, right):
        pl.semaphore_signal(barrier, inc=1, device_id={"elem": neighbour}, device_id_type=MESH)
    pl.semaphore_wait(barrier, 2)

    elements = order.shape[-1]
    lanes = lax.broadcasted_iota(jnp.int32, (elements, elements), 0)
    chosen = jnp.where(order[...] == lanes, 1.0, 0.0).astype(jnp.bfloat16)
    to_brick_matrix = jnp.concatenate([chosen, chosen], axis=1)
    to_slot_matrix = jnp.concatenate([chosen, chosen], axis=0)

    def to_brick(values):
        return lax.dot_general(
            jnp.concatenate(halves(values), axis=1),
            to_brick_matrix,
            (((1,), (1,)), ((), ())),
            preferred_element_type=jnp.float32,
        )

    def exchange(slot, rows):
        copies = []
        for side, target in ((0, right), (1, left)):
            copy = pltpu.make_async_remote_copy(
                src_ref=send.at[slot, side, pl.ds(0, rows)],
                dst_ref=recv.at[slot, side, pl.ds(0, rows)],
                send_sem=send_sem.at[slot, side],
                recv_sem=recv_sem.at[slot, side],
                device_id={"elem": target},
                device_id_type=MESH,
            )
            copy.start()
            copies.append(copy)
        return copies

    brick_mass = {}
    for i in (0, ORDER, *range(1, ORDER)):
        rows = slice(i * PLANE, (i + 1) * PLANE)
        weight = to_brick(mass[rows, :])
        for m in range(members + 1):
            value = weight if m == members else weight * to_brick(scalars[m, rows, :])
            if i in (0, ORDER):
                store_assembled(send.at[1, 0 if i == ORDER else 1], m * PLANE, value)
            else:
                store_assembled(work, (m * EXTENT + i) * PLANE, value)
        if i == ORDER:
            copies = exchange(1, (members + 1) * PLANE)
    for r in range(3):
        for i in range(EXTENT):
            rows = slice(i * PLANE, (i + 1) * PLANE)
            speed[r, rows, :] = to_brick(transport[r, rows, :])
    for copy in copies:
        copy.wait()
    for i in range(EXTENT):
        rows = slice(i * PLANE, (i + 1) * PLANE)

        def summed(m):
            if i == 0:
                part = slice(m * PLANE, (m + 1) * PLANE)
                return send[1, 1, part, :] + recv[1, 0, part, :]
            if i == ORDER:
                part = slice(m * PLANE, (m + 1) * PLANE)
                return send[1, 0, part, :] + recv[1, 1, part, :]
            return work[(m * EXTENT + i) * PLANE : (m * EXTENT + i + 1) * PLANE, :]

        scale = 1.0 / summed(members)
        for r in range(3):
            speed[r, rows, :] = -speed[r, rows, :] * scale
        for m in range(members):
            part = slice((m * EXTENT + i) * PLANE, (m * EXTENT + i + 1) * PLANE)
            value = summed(m) * scale
            current[0, part, :] = value
            base[part, :] = value
            total[part, :] = value

    derivative = gll_derivative(ORDER)
    half = EXTENT // 2

    def stage(index, carry):
        slot = lax.rem(index, 2)
        step = lax.rem(index, 4)
        last = step == 3
        weight = jnp.where(jnp.logical_or(step == 0, last), time_step / 6.0, time_step / 3.0)
        reach = jnp.where(step == 2, time_step, 0.5 * time_step)

        def plane(m, i):
            return current[slot, (m * EXTENT + i) * PLANE : (m * EXTENT + i + 1) * PLANE, :]

        def in_plane(i):
            stacked = []
            for m in range(members):
                high, low = halves(plane(m, i))
                stacked.append(jnp.concatenate([high, low, high], axis=0))
            return jnp.dot(
                matrix[...],
                jnp.concatenate(stacked, axis=1),
                preferred_element_type=jnp.float32,
            )

        def pair(a):
            inside = {a: in_plane(a), ORDER - a: in_plane(ORDER - a)}
            for m in range(members):
                even = odd = None
                for i in range(half):
                    near, far = plane(m, i), plane(m, ORDER - i)
                    plus = float(derivative[a, i] + derivative[a, ORDER - i]) * 0.5
                    minus = float(derivative[a, i] - derivative[a, ORDER - i]) * 0.5
                    even_term = plus * (near + far)
                    odd_term = minus * (near - far)
                    even = even_term if even is None else even + even_term
                    odd = odd_term if odd is None else odd + odd_term
                for i, across in ((a, odd + even), (ORDER - a, odd - even)):
                    rows = slice(i * PLANE, (i + 1) * PLANE)
                    columns = slice(m * elements, (m + 1) * elements)
                    yield m, i, (
                        speed[0, rows, :] * across
                        + speed[1, rows, :] * inside[i][:PLANE, columns]
                        + speed[2, rows, :] * inside[i][PLANE:, columns]
                    )

        def advance(m, i, tendency):
            part = slice((m * EXTENT + i) * PLANE, (m * EXTENT + i + 1) * PLANE)
            start = base[part, :]
            summed = total[part, :] + weight * tendency
            total[part, :] = summed
            current[1 - slot, part, :] = jnp.where(last, summed, start + reach * tendency)
            base[part, :] = jnp.where(last, summed, start)

        for m, i, value in pair(0):
            store_assembled(send.at[slot, 0 if i == ORDER else 1], m * PLANE, value)
        copies = exchange(slot, members * PLANE)
        for a in range(1, half):
            for m, i, value in pair(a):
                store_assembled(work, (m * EXTENT + i) * PLANE, value)
            for m in range(members):
                for i in (a, ORDER - a):
                    advance(m, i, work[(m * EXTENT + i) * PLANE : (m * EXTENT + i + 1) * PLANE, :])
        for copy in copies:
            copy.wait()
        for m in range(members):
            part = slice(m * PLANE, (m + 1) * PLANE)
            advance(m, 0, send[slot, 1, part, :] + recv[slot, 0, part, :])
            advance(m, ORDER, send[slot, 0, part, :] + recv[slot, 1, part, :])
        return carry

    lax.fori_loop(0, 4 * SUBSTEPS, stage, 0)
    for m in range(members):
        out[m, :, :] = jnp.dot(
            jnp.concatenate(halves(total[m * NODES : (m + 1) * NODES, :]), axis=1),
            to_slot_matrix,
            preferred_element_type=jnp.float32,
        )


def per_device(scalars, transport, mass, element_order):
    members, nodes, elements = scalars.shape
    count = lax.axis_size("elem")
    whole = pl.BlockSpec(memory_space=pltpu.VMEM)
    return pl.pallas_call(
        functools.partial(kernel, count, members),
        out_shape=jax.ShapeDtypeStruct(scalars.shape, jnp.float32),
        in_specs=[whole] * 5,
        out_specs=whole,
        scratch_shapes=[
            pltpu.VMEM((3, nodes, elements), jnp.float32),
            pltpu.VMEM((2, members * nodes, elements), jnp.float32),
            pltpu.VMEM((members * nodes, elements), jnp.float32),
            pltpu.VMEM((members * nodes, elements), jnp.float32),
            pltpu.VMEM(((members + 1) * nodes, elements), jnp.float32),
            pltpu.VMEM((8, elements), jnp.float32),
            pltpu.VMEM((2, 2, (members + 1) * PLANE, elements), jnp.float32),
            pltpu.VMEM((2, 2, (members + 1) * PLANE, elements), jnp.float32),
            pltpu.SemaphoreType.DMA((2, 2)),
            pltpu.SemaphoreType.DMA((2, 2)),
        ],
        compiler_params=pltpu.CompilerParams(collective_id=0, has_side_effects=True),
    )(scalars, transport, mass, element_order, jnp.asarray(split_matrix()))


def solution(mesh):
    in_specs = (P("ens", None, "elem"), P(None, None, "elem"), P(None, "elem"), P("elem", None))
    out_specs = P("ens", None, "elem")
    return jax.shard_map(
        per_device, mesh=mesh, in_specs=in_specs, out_specs=out_specs, check_vma=False
    )
```

profile of v0, /device:TPU:0, one launch (start us, length us, event | category | flops | bytes accessed | tf_op | source)
XLA Modules:
  0.0 55.1 jit_solution(4287506677793207424)
XLA Ops:
  0.0 53.3 %shard_map.55 = f32[2,512,128]{2,1,0:T(8,128)} custom-call(f32[2,512,128]{2,1,0:T(8,128)} %scalars.1, f32[3,512,128]{2,1,0:T(8,128)} %transport.1, f32[512,128]{1,0:T(8,128)} %mass.1, s32[1,128]{1,0:T(1,128)} %order.1, bf16[128,192]{1,0:T(8,128)(2,1)} %constant.2.clone.matrix), custom_call_target="tpu_custom_call" | custom-call | tf_op jit(solution)/shard_map/pallas_call | solution.py:267
  53.3 1.9 %copy.7 = f32[2,512,128]{2,1,0:T(8,128)} copy(f32[2,512,128]{2,1,0:T(8,128)} %shard_map.55) | data formatting | bytes 1048576
where the time goes:
time: 55.3 us; the launch traced here: 55.1 us
  Pallas kernels  53.3 us (96%)
  local copies, waits for them, and re-layouts  1.87 us (3%)
    pallas_call x1, Pallas kernels, per_device(): pl.pallas_call(functools.partial(kernel, count, members), out_shape=jax.S...  53.3 us
    unnamed x1, local copies, waits for them, and re-layouts  1.87 us

commit v1 on v0

v1 whole, which is shorter than its diff:
```python
import functools

import jax
import jax.numpy as jnp
import numpy as np
from jax import lax
from jax.experimental import pallas as pl
from jax.experimental.pallas import tpu as pltpu
from jax.sharding import PartitionSpec as P

ORDER = 7
SUBSTEPS = 2
EX = 1
EY = 8
EZ = 16
EXTENT = ORDER + 1
PLANE = EXTENT * EXTENT
NODES = EXTENT * PLANE
MESH = pl.DeviceIdType.MESH


time_step = 0.015


def legendre_table(points, degree):
    table = np.zeros((points.shape[0], degree + 1))
    table[:, 0] = 1.0
    table[:, 1] = points
    for level in range(2, degree + 1):
        table[:, level] = (
            (2 * level - 1) * points * table[:, level - 1] - (level - 1) * table[:, level - 2]
        ) / level
    return table


def gll_derivative(degree):
    extent = degree + 1
    points = np.cos(np.pi * np.arange(extent) / degree)
    for sweep in range(60):
        table = legendre_table(points, degree)
        points = points - (points * table[:, degree] - table[:, degree - 1]) / (
            extent * table[:, degree]
        )
    points = points[::-1].copy()
    values = legendre_table(points, degree)[:, degree]
    matrix = np.zeros((extent, extent))
    for target in range(extent):
        for source in range(extent):
            if target != source:
                matrix[target, source] = values[target] / (
                    values[source] * (points[target] - points[source])
                )
    matrix[0, 0] = -degree * (degree + 1) / 4.0
    matrix[extent - 1, extent - 1] = degree * (degree + 1) / 4.0
    return matrix


def split_matrix():
    derivative = gll_derivative(ORDER).astype(np.float32)
    eye = np.eye(EXTENT, dtype=np.float32)
    full = np.concatenate([np.kron(derivative, eye), np.kron(eye, derivative)], axis=0)
    high = full.astype(jnp.bfloat16)
    low = (full - high.astype(np.float32)).astype(jnp.bfloat16)
    return np.concatenate([high, high, low], axis=1)


def halves(values):
    high = values.astype(jnp.bfloat16)
    low = (values - high.astype(jnp.float32)).astype(jnp.bfloat16)
    return high, low


def lane_forward(values, stride, length):
    total = values.shape[-1]
    near = pltpu.roll(values, total - stride, 1)
    if stride * length == total:
        return near
    coords = lax.broadcasted_iota(jnp.int32, values.shape, 1) // stride % length
    return jnp.where(coords < length - 1, near, pltpu.roll(values, stride * (length - 1), 1))


def lane_backward(values, stride, length):
    total = values.shape[-1]
    near = pltpu.roll(values, stride, 1)
    if stride * length == total:
        return near
    coords = lax.broadcasted_iota(jnp.int32, values.shape, 1) // stride % length
    return jnp.where(coords > 0, near, pltpu.roll(values, total - stride * (length - 1), 1))


def store_assembled(ref, row, values):
    low, high = values[:EXTENT], values[PLANE - EXTENT :]
    ref[row : row + EXTENT] = low + lane_backward(high, EZ, EY)
    ref[row + EXTENT : row + PLANE - EXTENT] = values[EXTENT : PLANE - EXTENT]
    ref[row + PLANE - EXTENT : row + PLANE] = high + lane_forward(low, EZ, EY)
    first = pl.ds(row, EXTENT, stride=EXTENT)
    last = pl.ds(row + ORDER, EXTENT, stride=EXTENT)
    k_low = ref[first, :]
    k_high = ref[last, :]
    ref[first, :] = k_low + lane_backward(k_high, 1, EZ)
    ref[last, :] = k_high + lane_forward(k_low, 1, EZ)


def store_lower(ref, row, values):
    low, high = values[:EXTENT], values[PLANE - EXTENT :]
    ref[row : row + EXTENT] = low + lane_backward(high, EZ, EY)
    ref[row + EXTENT : row + PLANE] = values[EXTENT:]
    first = pl.ds(row, EXTENT, stride=EXTENT)
    k_high = ref[pl.ds(row + ORDER, EXTENT, stride=EXTENT), :]
    ref[first, :] = ref[first, :] + lane_backward(k_high, 1, EZ)


def pack(source, row, target):
    for j in range(ORDER):
        target[j * ORDER : j * ORDER + EXTENT] = source[row + j * EXTENT : row + (j + 1) * EXTENT]


def add_packed(ref, row, packed):
    for j in range(ORDER):
        part = slice(row + j * EXTENT, row + (j + 1) * EXTENT)
        ref[part] = ref[part] + packed[j * ORDER : j * ORDER + EXTENT]
    k_low = ref[pl.ds(row, EXTENT, stride=EXTENT), :]
    ref[pl.ds(row + ORDER, EXTENT, stride=EXTENT), :] = lane_forward(k_low, 1, EZ)
    ref[row + PLANE - EXTENT : row + PLANE] = lane_forward(ref[row : row + EXTENT], EZ, EY)


def kernel(
    count, members, scalars, transport, mass, order, matrix, out,
    speed, current, base, total, work, send, recv, send_sem, recv_sem,
):
    me = lax.axis_index("elem")
    right, left = lax.rem(me + 1, count), lax.rem(me + count - 1, count)
    barrier = pltpu.get_barrier_semaphore()
    for neighbour in (left, right):
        pl.semaphore_signal(barrier, inc=1, device_id={"elem": neighbour}, device_id_type=MESH)

    elements = order.shape[-1]
    lanes = lax.broadcasted_iota(jnp.int32, (elements, elements), 0)
    chosen = jnp.where(order[...] == lanes, 1.0, 0.0).astype(jnp.bfloat16)
    to_brick_matrix = jnp.concatenate([chosen, chosen], axis=1)
    to_slot_matrix = jnp.concatenate([chosen, chosen], axis=0)

    def to_brick(values):
        return lax.dot_general(
            jnp.concatenate(halves(values), axis=1),
            to_brick_matrix,
            (((1,), (1,)), ((), ())),
            preferred_element_type=jnp.float32,
        )

    first_side = 1 - lax.rem(me, 2)
    sides = (first_side, 1 - first_side)

    def copies_of(slot, m):
        copies = []
        for side in sides:
            copies.append(
                pltpu.make_async_remote_copy(
                    src_ref=send.at[slot, m, side, pl.ds(0, ORDER * ORDER)],
                    dst_ref=recv.at[slot, m, side, pl.ds(0, ORDER * ORDER)],
                    send_sem=send_sem.at[slot, m, side],
                    recv_sem=recv_sem.at[slot, m, side],
                    device_id={"elem": side * left + (1 - side) * right},
                    device_id_type=MESH,
                )
            )
        return copies

    def start(slot, m):
        for copy in copies_of(slot, m):
            copy.start()

    def finish(slot, m):
        for copy in copies_of(slot, m):
            copy.wait()

    def row_of(m, i):
        return (m * EXTENT + i) * PLANE

    def rows_of(m, i):
        return slice(row_of(m, i), row_of(m, i) + PLANE)

    def plane_rows(i):
        return slice(i * PLANE, (i + 1) * PLANE)

    def put_face(slot, m, i, value):
        store_lower(work, row_of(m, i), value)
        pack(work, row_of(m, i), send.at[slot, m, 0 if i == ORDER else 1])

    def take_faces(slot, m):
        finish(slot, m)
        add_packed(work, row_of(m, 0), recv.at[slot, m, 0])
        add_packed(work, row_of(m, ORDER), recv.at[slot, m, 1])

    weights = {}
    for i in (0, ORDER):
        weights[i] = to_brick(mass[plane_rows(i), :])
        put_face(1, members, i, weights[i])
    pl.semaphore_wait(barrier, 2)
    start(1, members)
    for m in range(members):
        for i in (0, ORDER):
            put_face(1, m, i, weights[i] * to_brick(scalars[m, plane_rows(i), :]))
        start(1, m)
    for i in range(1, ORDER):
        weight = to_brick(mass[plane_rows(i), :])
        store_assembled(work, row_of(members, i), weight)
        for m in range(members):
            store_assembled(work, row_of(m, i), weight * to_brick(scalars[m, plane_rows(i), :]))
    for r in range(3):
        for i in range(EXTENT):
            speed[r, plane_rows(i), :] = to_brick(transport[r, plane_rows(i), :])

    def begin(m, i):
        value = work[rows_of(m, i), :] * work[rows_of(members, i), :]
        current[0, rows_of(m, i), :] = value
        base[rows_of(m, i), :] = value
        total[rows_of(m, i), :] = value

    def scale(i):
        inverse = 1.0 / work[rows_of(members, i), :]
        work[rows_of(members, i), :] = inverse
        for r in range(3):
            speed[r, plane_rows(i), :] = -speed[r, plane_rows(i), :] * inverse

    for i in range(1, ORDER):
        scale(i)
        for m in range(members):
            begin(m, i)
    take_faces(1, members)
    scale(0)
    scale(ORDER)

    derivative = gll_derivative(ORDER)
    half = EXTENT // 2

    def pair(slot, m, a):
        def plane(i):
            return current[slot, rows_of(m, i), :]

        even = odd = None
        for i in range(half):
            near, far = plane(i), plane(ORDER - i)
            plus = float(derivative[a, i] + derivative[a, ORDER - i]) * 0.5
            minus = float(derivative[a, i] - derivative[a, ORDER - i]) * 0.5
            even_term = plus * (near + far)
            odd_term = minus * (near - far)
            even = even_term if even is None else even + even_term
            odd = odd_term if odd is None else odd + odd_term
        stacked = []
        for i in (a, ORDER - a):
            high, low = halves(plane(i))
            stacked.append(jnp.concatenate([high, low, high], axis=0))
        inside = jnp.dot(
            matrix[...],
            jnp.concatenate(stacked, axis=1),
            preferred_element_type=jnp.float32,
        )
        for place, (i, across) in enumerate(((a, odd + even), (ORDER - a, odd - even))):
            columns = slice(place * elements, (place + 1) * elements)
            yield i, (
                speed[0, plane_rows(i), :] * across
                + speed[1, plane_rows(i), :] * inside[:PLANE, columns]
                + speed[2, plane_rows(i), :] * inside[PLANE:, columns]
            )

    def advance(index, m, i):
        step = lax.rem(index, 4)
        last = step == 3
        weight = jnp.where(jnp.logical_or(step == 0, last), time_step / 6.0, time_step / 3.0)
        reach = jnp.where(step == 2, time_step, 0.5 * time_step)
        tendency = work[rows_of(m, i), :]
        origin = base[rows_of(m, i), :]
        summed = total[rows_of(m, i), :] + weight * tendency
        total[rows_of(m, i), :] = summed
        current[1 - lax.rem(index, 2), rows_of(m, i), :] = jnp.where(
            last, summed, origin + reach * tendency
        )
        base[rows_of(m, i), :] = jnp.where(last, summed, origin)

    def close(index, m):
        take_faces(lax.rem(index, 2), m)
        advance(index, m, 0)
        advance(index, m, ORDER)

    def open_faces(index, m):
        slot = lax.rem(index, 2)
        for i, value in pair(slot, m, 0):
            put_face(slot, m, i, value)
        start(slot, m)

    def interior(index):
        for m in range(members):
            for a in range(1, half):
                for i, value in pair(lax.rem(index, 2), m, a):
                    store_assembled(work, row_of(m, i), value)
                    advance(index, m, i)

    for m in range(members):
        take_faces(1, m)
        begin(m, 0)
        begin(m, ORDER)
        open_faces(0, m)
    interior(0)

    def stage(index, carry):
        for m in range(members):
            close(index - 1, m)
            open_faces(index, m)
        interior(index)
        return carry

    final = 4 * SUBSTEPS - 1
    lax.fori_loop(1, final + 1, stage, 0)
    for m in range(members):
        close(final, m)
        out[m, :, :] = jnp.dot(
            jnp.concatenate(halves(total[m * NODES : (m + 1) * NODES, :]), axis=1),
            to_slot_matrix,
            preferred_element_type=jnp.float32,
        )


def per_device(scalars, transport, mass, element_order):
    members, nodes, elements = scalars.shape
    count = lax.axis_size("elem")
    whole = pl.BlockSpec(memory_space=pltpu.VMEM)
    return pl.pallas_call(
        functools.partial(kernel, count, members),
        out_shape=jax.ShapeDtypeStruct(scalars.shape, jnp.float32),
        in_specs=[whole] * 5,
        out_specs=whole,
        scratch_shapes=[
            pltpu.VMEM((3, nodes, elements), jnp.float32),
            pltpu.VMEM((2, members * nodes, elements), jnp.float32),
            pltpu.VMEM((members * nodes, elements), jnp.float32),
            pltpu.VMEM((members * nodes, elements), jnp.float32),
            pltpu.VMEM(((members + 1) * nodes, elements), jnp.float32),
            pltpu.VMEM((2, members + 1, 2, PLANE - EXTENT, elements), jnp.float32),
            pltpu.VMEM((2, members + 1, 2, PLANE - EXTENT, elements), jnp.float32),
            pltpu.SemaphoreType.DMA((2, members + 1, 2)),
            pltpu.SemaphoreType.DMA((2, members + 1, 2)),
        ],
        compiler_params=pltpu.CompilerParams(collective_id=0, has_side_effects=True),
    )(scalars, transport, mass, element_order, jnp.asarray(split_matrix()))


def solution(mesh):
    in_specs = (P("ens", None, "elem"), P(None, None, "elem"), P(None, "elem"), P("elem", None))
    out_specs = P("ens", None, "elem")
    return jax.shard_map(
        per_device, mesh=mesh, in_specs=in_specs, out_specs=out_specs, check_vma=False
    )
```

time: 55.3 us -> 51.6 us (0.933)
  Pallas kernels: 53.3 us -> 49.5 us
    pallas_call x1, Pallas kernels: 53.3 us -> 49.5 us  [per_device(): pl.pallas_call(functools.partial(kernel, count, members), out_shape=jax.S...]
where the time goes in v1:
time: 51.6 us; the launch traced here: 51.4 us
  Pallas kernels  49.5 us (96%)
  local copies, waits for them, and re-layouts  1.87 us (4%)
    pallas_call x1, Pallas kernels, per_device(): pl.pallas_call(functools.partial(kernel, count, members), out_shape=jax.S...  49.5 us
    unnamed x1, local copies, waits for them, and re-layouts  1.87 us

profile of v1, /device:TPU:0, one launch (start us, length us, event | category | flops | bytes accessed | tf_op | source)
XLA Modules:
  0.0 51.4 jit_solution(13335275091358603803)
XLA Ops:
  0.0 49.5 %shard_map.55 = f32[2,512,128]{2,1,0:T(8,128)} custom-call(f32[2,512,128]{2,1,0:T(8,128)} %scalars.1, f32[3,512,128]{2,1,0:T(8,128)} %transport.1, f32[512,128]{1,0:T(8,128)} %mass.1, s32[1,128]{1,0:T(1,128)} %order.1, bf16[128,192]{1,0:T(8,128)(2,1)} %constant.2.clone.matrix), custom_call_target="tpu_custom_call" | custom-call | tf_op jit(solution)/shard_map/pallas_call | solution.py:328
  49.5 1.9 %copy.7 = f32[2,512,128]{2,1,0:T(8,128)} copy(f32[2,512,128]{2,1,0:T(8,128)} %shard_map.55) | data formatting | bytes 1048576

commit v2 on v1

--- a/solution.py
+++ b/solution.py
@@ -125,9 +125,17 @@
 
 
 def kernel(
-    count, members, scalars, transport, mass, order, matrix, out,
-    speed, current, base, total, work, send, recv, send_sem, recv_sem,
+    count, members, scalars_in, transport_in, mass_in, order, matrix, total,
+    scalars, transport, mass, speed, current, base, work, send, recv, load_sem, send_sem, recv_sem,
 ):
+    loads = [
+        pltpu.make_async_copy(source, target, load_sem.at[place])
+        for place, (source, target) in enumerate(
+            ((mass_in, mass), (scalars_in, scalars), (transport_in, transport))
+        )
+    ]
+    for load in loads:
+        load.start()
     me = lax.axis_index("elem")
     right, left = lax.rem(me + 1, count), lax.rem(me + count - 1, count)
     barrier = pltpu.get_barrier_semaphore()
@@ -138,7 +146,6 @@
     lanes = lax.broadcasted_iota(jnp.int32, (elements, elements), 0)
     chosen = jnp.where(order[...] == lanes, 1.0, 0.0).astype(jnp.bfloat16)
     to_brick_matrix = jnp.concatenate([chosen, chosen], axis=1)
-    to_slot_matrix = jnp.concatenate([chosen, chosen], axis=0)
 
     def to_brick(values):
         return lax.dot_general(
@@ -192,12 +199,14 @@
         add_packed(work, row_of(m, 0), recv.at[slot, m, 0])
         add_packed(work, row_of(m, ORDER), recv.at[slot, m, 1])
 
+    loads[0].wait()
     weights = {}
     for i in (0, ORDER):
         weights[i] = to_brick(mass[plane_rows(i), :])
         put_face(1, members, i, weights[i])
     pl.semaphore_wait(barrier, 2)
     start(1, members)
+    loads[1].wait()
     for m in range(members):
         for i in (0, ORDER):
             put_face(1, m, i, weights[i] * to_brick(scalars[m, plane_rows(i), :]))
@@ -207,6 +216,7 @@
         store_assembled(work, row_of(members, i), weight)
         for m in range(members):
             store_assembled(work, row_of(m, i), weight * to_brick(scalars[m, plane_rows(i), :]))
+    loads[2].wait()
     for r in range(3):
         for i in range(EXTENT):
             speed[r, plane_rows(i), :] = to_brick(transport[r, plane_rows(i), :])
@@ -314,35 +324,58 @@
     lax.fori_loop(1, final + 1, stage, 0)
     for m in range(members):
         close(final, m)
-        out[m, :, :] = jnp.dot(
-            jnp.concatenate(halves(total[m * NODES : (m + 1) * NODES, :]), axis=1),
-            to_slot_matrix,
-            preferred_element_type=jnp.float32,
-        )
+
+
+def slot_kernel(order, values, out):
+    elements = order.shape[-1]
+    lanes = lax.broadcasted_iota(jnp.int32, (elements, elements), 0)
+    chosen = jnp.where(order[...] == lanes, 1.0, 0.0).astype(jnp.bfloat16)
+    out[...] = jnp.dot(
+        jnp.concatenate(halves(values[...]), axis=1),
+        jnp.concatenate([chosen, chosen], axis=0),
+        preferred_element_type=jnp.float32,
+    )
 
 
 def per_device(scalars, transport, mass, element_order):
     members, nodes, elements = scalars.shape
     count = lax.axis_size("elem")
     whole = pl.BlockSpec(memory_space=pltpu.VMEM)
-    return pl.pallas_call(
+    rows = members * nodes
+    outside = pl.BlockSpec(memory_space=pltpu.HBM)
+    final = pl.pallas_call(
         functools.partial(kernel, count, members),
-        out_shape=jax.ShapeDtypeStruct(scalars.shape, jnp.float32),
-        in_specs=[whole] * 5,
+        out_shape=jax.ShapeDtypeStruct((rows, elements), jnp.float32),
+        in_specs=[outside] * 3 + [whole] * 2,
         out_specs=whole,
         scratch_shapes=[
+            pltpu.VMEM(scalars.shape, jnp.float32),
+            pltpu.VMEM(transport.shape, jnp.float32),
+            pltpu.VMEM(mass.shape, jnp.float32),
             pltpu.VMEM((3, nodes, elements), jnp.float32),
-            pltpu.VMEM((2, members * nodes, elements), jnp.float32),
-            pltpu.VMEM((members * nodes, elements), jnp.float32),
-            pltpu.VMEM((members * nodes, elements), jnp.float32),
-            pltpu.VMEM(((members + 1) * nodes, elements), jnp.float32),
+            pltpu.VMEM((2, rows, elements), jnp.float32),
+            pltpu.VMEM((rows, elements), jnp.float32),
+            pltpu.VMEM((rows + nodes, elements), jnp.float32),
             pltpu.VMEM((2, members + 1, 2, PLANE - EXTENT, elements), jnp.float32),
             pltpu.VMEM((2, members + 1, 2, PLANE - EXTENT, elements), jnp.float32),
+            pltpu.SemaphoreType.DMA((3,)),
             pltpu.SemaphoreType.DMA((2, members + 1, 2)),
             pltpu.SemaphoreType.DMA((2, members + 1, 2)),
         ],
-        compiler_params=pltpu.CompilerParams(collective_id=0, has_side_effects=True),
+        compiler_params=pltpu.CompilerParams(
+            collective_id=0, has_side_effects=True, vmem_limit_bytes=24 * 1024 * 1024
+        ),
     )(scalars, transport, mass, element_order, jnp.asarray(split_matrix()))
+    block = pl.BlockSpec((nodes // 2, elements), lambda step: (step, 0))
+    slots = pl.pallas_call(
+        slot_kernel,
+        out_shape=jax.ShapeDtypeStruct((rows, elements), jnp.float32),
+        grid=(2 * members,),
+        in_specs=[pl.BlockSpec(element_order.shape, lambda step: (0, 0)), block],
+        out_specs=block,
+        compiler_params=pltpu.CompilerParams(vmem_limit_bytes=8 * 1024 * 1024),
+    )(element_order, final)
+    return slots.reshape(scalars.shape)
 
 
 def solution(mesh):

time: 51.6 us -> 54.1 us (1.048)
  local copies, waits for them, and re-layouts: 1.87 us -> 4.62 us
    unnamed x1 -> x10, local copies, waits for them, and re-layouts: 1.87 us -> 4.62 us
    pallas_call x1, Pallas kernels: 49.5 us -> 47.3 us  [per_device(): pl.pallas_call(functools.partial(kernel, count, members), out_shape=jax.S...]
    pallas_call x0 -> x1, Pallas kernels: none -> 1.88 us  [per_device(): pl.pallas_call(slot_kernel, out_shape=jax.ShapeDtypeStruct((rows, element...]
where the time goes in v2:
time: 54.1 us; the launch traced here: 53.8 us
  Pallas kernels  49.2 us (91%)
  local copies, waits for them, and re-layouts  4.62 us (9%)
    pallas_call x1, Pallas kernels, per_device(): pl.pallas_call(functools.partial(kernel, count, members), out_shape=jax.S...  47.3 us
    unnamed x10, local copies, waits for them, and re-layouts  4.62 us
    pallas_call x1, Pallas kernels, per_device(): pl.pallas_call(slot_kernel, out_shape=jax.ShapeDtypeStruct((rows, element...  1.88 us

profile of v2, /device:TPU:0, one launch (start us, length us, event | category | flops | bytes accessed | tf_op | source)
XLA Modules:
  0.0 53.8 jit_solution(2169803038871014221)
XLA Ops:
  0.0 0.0 copy-start
  0.0 1.1 %copy-done = f32[3,512,128]{2,1,0:T(8,128)S(1)} copy-done((f32[3,512,128]{2,1,0:T(8,128)S(1)}, f32[3,512,128]{2,1,0:T(8,128)}, u32[]{:S(2)}) %copy-start) | copy-done | bytes 786456
  1.1 0.0 copy-start.1
  1.1 1.0 %copy-done.1 = f32[2,512,128]{2,1,0:T(8,128)S(1)} copy-done((f32[2,512,128]{2,1,0:T(8,128)S(1)}, f32[2,512,128]{2,1,0:T(8,128)}, u32[]{:S(2)}) %copy-start.1) | copy-done | bytes 524312
  2.2 0.0 copy-start.2
  2.2 0.9 %copy-done.2 = f32[512,128]{1,0:T(8,128)S(1)} copy-done((f32[512,128]{1,0:T(8,128)S(1)}, f32[512,128]{1,0:T(8,128)}, u32[]{:S(2)}) %copy-start.2) | copy-done | bytes 262168
  3.1 0.0 copy-start.3
  3.1 0.8 %copy-done.3 = bf16[128,192]{1,0:T(8,128)(2,1)S(1)} copy-done((bf16[128,192]{1,0:T(8,128)(2,1)S(1)}, bf16[128,192]{1,0:T(8,128)(2,1)}, u32[]{:S(2)}) %copy-start.3) | copy-done | bytes 49176
  4.0 0.0 copy-start.4
  4.0 0.7 %copy-done.4 = s32[1,128]{1,0:T(1,128)S(1)} copy-done((s32[1,128]{1,0:T(1,128)S(1)}, s32[1,128]{1,0:T(1,128)}, u32[]{:S(2)}) %copy-start.4) | copy-done | bytes 536
  4.6 47.3 %shard_map.55.values = f32[1024,128]{1,0:T(8,128)S(1)} custom-call(f32[2,512,128]{2,1,0:T(8,128)S(1)} %copy-done.1, f32[3,512,128]{2,1,0:T(8,128)S(1)} %copy-done, f32[512,128]{1,0:T(8,128)S(1)} %copy-done.2, s32[1,128]{1,0:T(1,128)S(1)} %copy-done.4, bf16[128,192]{1,0:T(8,128)(2,1)S(1)} %copy-done.3), custom_call_target="tpu_custom_call" | custom-call | tf_op jit(solution)/shard_map/pallas_call | solution.py:346
  51.9 1.9 %shard_map.56 = f32[1024,128]{1,0:T(8,128)} custom-call(s32[1,128]{1,0:T(1,128)S(1)} %copy-done.4, f32[1024,128]{1,0:T(8,128)S(1)} %shard_map.55.values), custom_call_target="tpu_custom_call" | custom-call | tf_op jit(solution)/shard_map/pallas_call | solution.py:370
Async XLA Ops:
  0.0 1.1 %copy-start = (f32[3,512,128]{2,1,0:T(8,128)S(1)}, f32[3,512,128]{2,1,0:T(8,128)}, u32[]{:S(2)}) copy-start(f32[3,512,128]{2,1,0:T(8,128)} %transport_in.1) | copy-start | bytes 2359300
  1.1 1.0 %copy-start.1 = (f32[2,512,128]{2,1,0:T(8,128)S(1)}, f32[2,512,128]{2,1,0:T(8,128)}, u32[]{:S(2)}) copy-start(f32[2,512,128]{2,1,0:T(8,128)} %scalars_in.1) | copy-start | bytes 1572868
  2.2 0.9 %copy-start.2 = (f32[512,128]{1,0:T(8,128)S(1)}, f32[512,128]{1,0:T(8,128)}, u32[]{:S(2)}) copy-start(f32[512,128]{1,0:T(8,128)} %mass_in.1) | copy-start | bytes 786436
  3.1 0.8 %copy-start.3 = (bf16[128,192]{1,0:T(8,128)(2,1)S(1)}, bf16[128,192]{1,0:T(8,128)(2,1)}, u32[]{:S(2)}) copy-start(bf16[128,192]{1,0:T(8,128)(2,1)} %constant.2.clone.matrix) | copy-start | bytes 147460
  4.0 0.7 %copy-start.4 = (s32[1,128]{1,0:T(1,128)S(1)}, s32[1,128]{1,0:T(1,128)}, u32[]{:S(2)}) copy-start(s32[1,128]{1,0:T(1,128)} %order.3) | copy-start | bytes 1540
